TPU v7x, 32 devices: a 4x4x1 block of a 4x4x8 slice. The times are simulated.
32 devices in a mesh: dp: 1 (over z), tp: 32 (over y, x, core).
Axes of the slice: x: 4, y: 4, z: 1, core: 2. Of those that a mesh axis runs over, the one named last changes fastest.
The devices are a block of a 4x4x8 slice.
Arguments:
- hidden: bfloat16 [512, 4, 8192], P('dp')
- w_head: bfloat16 [8192, 32000], P(None, 'tp')
- q_draft: float32 [512, 3, 32000], P(('dp', 'tp'))
- x_draft: int32 [512, 3], P('dp')
Outputs:
- output 1: float32 [512, 3], P(('dp', 'tp'))
- output 2: float32 [512], P(('dp', 'tp'))
- output 3: float32 [512, 3, 32000], P(('dp', 'tp'))
- output 4: float32 [512, 32000], P(('dp', 'tp'))
All inputs are finite; a program needn't handle non-finite values.
Results may differ from a plain program's by a relative error of at most 0.001.
Values are sent between devices in bfloat16 or wider.
A program may use at most 768 MiB of HBM per device.

v0:
```python
import jax
import jax.numpy as jnp
from jax import lax
from jax.sharding import PartitionSpec as P

INV_TEMP = 1.25


def verify_rows(logits, q_rows, x_rows):
    draft_len = q_rows.shape[1]
    row_peak = jnp.max(logits, axis=-1, keepdims=True)
    exp_vals = jnp.exp(logits - row_peak)
    target_p = exp_vals / jnp.sum(exp_vals, axis=-1, keepdims=True)
    draft_p = target_p[:, :draft_len]
    p_pick = jnp.take_along_axis(draft_p, x_rows[:, :, None], axis=2)[:, :, 0]
    q_pick = jnp.take_along_axis(q_rows, x_rows[:, :, None], axis=2)[:, :, 0]
    accept = jnp.minimum(1.0, p_pick / q_pick)
    expected = jnp.sum(jnp.cumprod(accept, axis=1), axis=1)
    excess = jnp.maximum(draft_p - q_rows, 0.0)
    residual = excess / jnp.sum(excess, axis=-1, keepdims=True)
    return accept, expected, residual, target_p[:, draft_len]


def solution(mesh):
    def local_step(hidden, w_shard, q_rows, x_group):
        seq_dev = q_rows.shape[0]
        logits = jnp.einsum("bjd,dv->bjv", hidden, w_shard, preferred_element_type=jnp.float32) * INV_TEMP
        seq_logits = lax.all_to_all(logits, "tp", 0, 2, tiled=True)
        tp_rank = lax.axis_index("tp")
        x_rows = lax.dynamic_slice_in_dim(x_group, tp_rank * seq_dev, seq_dev, axis=0)
        return verify_rows(seq_logits, q_rows, x_rows)

    return jax.shard_map(local_step, mesh=mesh,
                         in_specs=(P("dp", None, None), P(None, "tp"), P(("dp", "tp"), None, None), P("dp", None)),
                         out_specs=(P(("dp", "tp"), None), P(("dp", "tp")), P(("dp", "tp"), None, None), P(("dp", "tp"), None)),
                         check_vma=False)
```

profile of v0, /device:TPU:103, one launch (start us, length us, event | category | flops | bytes accessed | tf_op | source)
XLA Modules:
  0.0 267.9 jit_solution(8625821378418790664)
XLA Ops:
  0.6 73.4 %broadcast_multiply_fusion = f32[512,4,1000]{0,2,1:T(8,128)} fusion(bf16[8192,1000]{0,1:T(8,128)(2,1)} %param.7, bf16[512,4,8192]{2,1,0:T(4,128)(2,1)} %param.6), kind=kOutput, calls=%fused_computation.8 | convolution fusion | flops 33556480000 | bytes 58130432 | tf_op jit(solution)/shard_map/bjd,dv->bjv/dot_general | solution.py:27
  74.0 10.4 %copy.26 = f32[512,4,1000]{2,1,0:T(4,128)} copy(f32[512,4,1000]{0,2,1:T(8,128)} %broadcast_multiply_fusion) | data formatting | bytes 16384000 | tf_op jit(solution)/shard_map/mul | solution.py:27
  84.5 0.0 copy-start.3
  84.5 8.0 %all-to-all-start = ((f32[512,4,1000]{2,1,0:T(4,128)}), f32[512,4,1000]{2,1,0:T(4,128)}, u32[]{:S(2)}, u32[]{:S(2)}) async-start(f32[512,4,1000]{2,1,0:T(4,128)} %copy.26), calls=%async_computation | async-start | bytes 16777216 | tf_op jit(solution)/shard_map/all_to_all | solution.py:28
  92.5 0.0 copy-done.3
  92.5 0.1 fusion.13
  92.6 0.1 copy.30
  92.7 0.1 reshape.51
  92.8 2.5 gather_fusion.1
  95.3 0.1 reshape.60
  95.4 0.1 copy.34
  95.5 110.1 %all-to-all-done = f32[512,4,1000]{2,1,0:T(4,128)} async-done(((f32[512,4,1000]{2,1,0:T(4,128)}), f32[512,4,1000]{2,1,0:T(4,128)}, u32[]{:S(2)}, u32[]{:S(2)}) %all-to-all-start) | async-done | bytes 8192032 | tf_op jit(solution)/shard_map/all_to_all | solution.py:28
  205.6 8.2 %copy.27 = f32[512,4,1000]{2,0,1:T(8,128)S(1)} copy(f32[512,4,1000]{2,1,0:T(4,128)} %all-to-all-done) | data formatting | bytes 16384000 | tf_op jit(solution)/shard_map/all_to_all | solution.py:28
  213.8 0.0 copy-start
  213.9 3.2 %copy-done = f32[512,4,1000]{2,0,1:T(8,128)} copy-done((f32[512,4,1000]{2,0,1:T(8,128)}, f32[512,4,1000]{2,0,1:T(8,128)S(1)}, u32[]{:S(2)}) %copy-start) | copy-done | bytes 8192024
  217.1 8.1 %copy.28 = f32[16,4,32,1000]{3,2,0,1:T(8,128)} copy(f32[16,4,32,1000]{3,0,2,1:T(8,128)S(1)} %bitcast.30) | data formatting | bytes 16384000 | tf_op jit(solution)/shard_map/all_to_all | solution.py:28
  225.1 4.0 %reduce_max.9 = f32[16,4]{0,1:T(4,128)S(1)} reduce(f32[16,4,32,1000]{3,0,2,1:T(8,128)} %bitcast.31, f32[]{:T(128)} %constant.4.clone.1), dimensions={2,3}, to_apply=%region_0.0 | reduce | flops 2047936 | bytes 8192260 | tf_op jit(solution)/shard_map/reduce_max | solution.py:11
  229.1 5.0 %exponential_reduce_fusion = f32[16,4]{0,1:T(4,128)S(1)} fusion(f32[16,4,32,1000]{3,0,2,1:T(8,128)} %bitcast.32, f32[16,4]{0,1:T(4,128)S(1)} %reduce_max.9), kind=kLoop, calls=%fused_computation.5 | loop fusion | flops 4095936 | bytes 8192512 | tf_op jit(solution)/shard_map/reduce_sum | solution.py:13
  234.1 0.0 slice-start
  234.1 9.3 %all_to_all.16 = f32[16,4,32000]{2,0,1:T(8,128)} reshape(f32[16,4,32,1000]{3,2,0,1:T(8,128)} %copy.28) | data formatting | bytes 16384000 | tf_op jit(solution)/shard_map/all_to_all | solution.py:28
  243.4 0.0 slice-start.1
  243.4 4.6 %exponential_divide_fusion = f32[16,4,32000]{2,0,1:T(8,128)S(1)} fusion(f32[16,4,32000]{2,0,1:T(8,128)} %all_to_all.16, f32[16,4]{0,1:T(4,128)S(1)} %exponential_reduce_fusion, f32[16,4]{0,1:T(4,128)S(1)} %reduce_max.9), kind=kLoop, calls=%fused_computation.6 | loop fusion | flops 4096000 | bytes 16384512 | tf_op jit(solution)/shard_map/div | solution.py:13
  248.0 0.0 copy-start.1
  248.0 6.6 %fusion.7 = f32[16,3]{0,1:T(4,128)S(1)} fusion(f32[16,3,32000]{2,0,1:T(8,128)} %param.8, f32[16,4,32000]{2,0,1:T(8,128)S(1)} %exponential_divide_fusion), kind=kLoop, calls=%fused_computation.10 | loop fusion | flops 4607952 | bytes 12288192 | tf_op jit(solution)/shard_map/reduce_sum | solution.py:20
  254.7 0.0 copy-done.1
  254.7 1.4 slice_bitcast_fusion
  256.1 0.0 slice-done
  256.1 0.0 slice-done.1
  256.1 8.4 %broadcast_divide_fusion = (f32[16,3,32000]{2,0,1:T(8,128)}, f32[16,3,32000]{2,0,1:T(8,128)}) fusion(f32[16,3]{0,1:T(4,128)S(1)} %fusion.7, f32[16,3,32000]{2,0,1:T(8,128)S(1)} %bitcast.34, f32[16,4,32000]{2,0,1:T(8,128)} %copy-done.1), kind=kLoop, calls=%fused_computation.9 | loop fusion | flops 4608000 | bytes 24576192 | tf_op jit(solution)/shard_map/div | solution.py:20
  264.5 2.5 gather_fusion
  267.0 0.1 reshape.54
  267.1 0.1 copy.31
  267.2 0.1 minimum_bitcast_fusion
  267.3 0.0 copy-start.2
  267.3 0.5 reduce_sum.28
  267.9 0.0 copy-done.2
  (6 shorter events, 0.1 us)
Async XLA Ops:
  84.5 8.0 %copy-start.3 = (s32[512,3]{0,1:T(4,128)S(1)}, s32[512,3]{0,1:T(4,128)}, u32[]{:S(2)}) copy-start(s32[512,3]{0,1:T(4,128)} %param.9) | copy-start | bytes 18436
  84.5 121.1 %all-to-all-start = ((f32[512,4,1000]{2,1,0:T(4,128)}), f32[512,4,1000]{2,1,0:T(4,128)}, u32[]{:S(2)}, u32[]{:S(2)}) async-start(f32[512,4,1000]{2,1,0:T(4,128)} %copy.26), calls=%async_computation | async-start | bytes 16777216 | tf_op jit(solution)/shard_map/all_to_all | solution.py:28
  213.8 3.2 %copy-start = (f32[512,4,1000]{2,0,1:T(8,128)}, f32[512,4,1000]{2,0,1:T(8,128)S(1)}, u32[]{:S(2)}) copy-start(f32[512,4,1000]{2,0,1:T(8,128)S(1)} %copy.27) | copy-start | bytes 24576004
  234.1 22.0 %slice-start = ((s8[6144000]{0:T(1024)(128)(4,1)}), s8[1949696]{0:T(1024)(128)(4,1)S(1)}, s32[]{:S(2)}) async-start(s8[6144000]{0:T(1024)(128)(4,1)} %bitcast.33), calls=%async_computation.1 | async-start | bytes 3899392
  243.4 12.7 %slice-start.1 = ((s8[6144000]{0:T(1024)(128)(4,1)}), s8[4194304]{0:T(1024)(128)(4,1)S(1)}, s32[]{:S(2)}) async-start(s8[6144000]{0:T(1024)(128)(4,1)} %bitcast.33), calls=%async_computation.2 | async-start | bytes 8388608
  248.0 6.7 %copy-start.1 = (f32[16,4,32000]{2,0,1:T(8,128)}, f32[16,4,32000]{2,0,1:T(8,128)S(1)}, u32[]{:S(2)}) copy-start(f32[16,4,32000]{2,0,1:T(8,128)S(1)} %exponential_divide_fusion) | copy-start | bytes 24576004
  267.3 0.6 copy-start.2
where the time goes:
time: 269 us; the launch traced here: 268 us
  waiting for transfers between devices  110 us (41%)
  matrix products  73.4 us (27%)
  local copies, waits for them, and re-layouts  46.3 us (17%)
  other arithmetic  29.4 us (11%)
  starting transfers between devices  7.99 us (3%)
    all_to_all x1, waiting for transfers between devices, local_step(): seq_logits = lax.all_to_all(logits, 'tp', 0, 2, tiled=True)  110 us
    dot_general x1, matrix products, local_step(): jnp.einsum('bjd,dv->bjv', hidden, w_shard, preferred_element_type=jnp.flo...  73.4 us
    all_to_all x3, local copies, waits for them, and re-layouts, local_step(): seq_logits = lax.all_to_all(logits, 'tp', 0, 2, tiled=True)  25.6 us
    mul x1, local copies, waits for them, and re-layouts, local_step(): jnp.einsum('bjd,dv->bjv', hidden, w_shard, preferred_element_type=jnp.flo...  10.4 us
    div x1, other arithmetic, verify_rows(): residual = excess / jnp.sum(excess, axis=-1, keepdims=True)  8.38 us
    all_to_all x1, starting transfers between devices, local_step(): seq_logits = lax.all_to_all(logits, 'tp', 0, 2, tiled=True)  7.99 us
    reduce_sum x1, other arithmetic, verify_rows(): residual = excess / jnp.sum(excess, axis=-1, keepdims=True)  6.65 us
  transfers between devices with their start and end apart: 1, of which 1 were waited for; matrix products, arithmetic and copies ran while one was open for 1% of the time, Pallas kernels for 0%

commit v1 on v0

v1 whole, which is shorter than its diff:
```python
import functools
import math

import jax
import jax.numpy as jnp
from jax import lax
from jax.experimental import pallas as pl
from jax.experimental.pallas import tpu as pltpu
from jax.sharding import PartitionSpec as P

INV_TEMP = 1.25
LANES = 128
TOP_CODE = 65535.0
MAX_SPAN = 87.0
LOG2E = math.log2(math.e)


def chip_order(side):
    offsets = [(dy, dx) for dy in range(side) for dx in range(side)]
    back = lambda o: (-o[0] % side, -o[1] % side)
    reach = lambda o: min(o[0], side - o[0]) + min(o[1], side - o[1])
    two_way = sorted((o for o in offsets if o < back(o)), key=lambda o: (-reach(o), o))
    one_way = sorted((o for o in offsets if o == back(o)), key=lambda o: -reach(o))
    pairs = [(o, back(o)) for o in two_way]
    pairs += [(one_way[i], one_way[i + 1]) for i in range(0, len(one_way), 2)]
    return pairs


def logits_kernel(n, tp, h_ref, w_ref, code_ref, stat_ref, wbuf, hbuf, acc, sbuf, stcol, stbuf,
                  wsem, hsem, code_send, code_recv, stat_send, stat_recv, self_sem):
    cores = 2
    side = math.isqrt(n // cores)
    pairs = chip_order(side)
    n_steps = len(pairs)
    me = lax.axis_index(tp)
    my_chip = me // cores
    my_y, my_x = my_chip // side, my_chip % side
    cols, depth = w_ref.shape
    half = code_ref.shape[2]
    seqs, tiles, pos, _ = h_ref.shape
    chip_seqs = seqs // (n // cores)
    dev_rows = chip_seqs // cores * pos
    blk_seqs = dev_rows // pos
    rows = 2 * chip_seqs * pos
    slices = wsem.shape[0]
    span = tiles // slices

    def chip_at(dy, dx):
        return ((my_y + dy) % side) * side + (my_x + dx) % side

    def pack(column):
        total = 0
        for value in reversed(column):
            total = total * side + value
        return total

    tables = tuple(pack([pair[a][b] for pair in pairs]) for a in range(2) for b in range(2))

    def fetch(slot, k, chips):
        for a in range(2):
            pltpu.make_async_copy(
                h_ref.at[pl.ds(chips[a] * chip_seqs, chip_seqs), pl.ds(k * span, span)],
                hbuf.at[slot, pl.ds(a * chip_seqs, chip_seqs), pl.ds(k * span, span)],
                hsem.at[slot, k]).start()

    first = tuple(chip_at(*pairs[0][a]) for a in range(2))
    for k in range(slices):
        cut = pl.ds(k * span * LANES, span * LANES)
        pltpu.make_async_copy(w_ref.at[:, cut], wbuf.at[:, cut], wsem.at[k]).start()
        fetch(0, k, first)

    barrier = pltpu.get_barrier_semaphore()

    def tell(i, carry):
        pl.semaphore_signal(barrier, inc=1, device_id={tp: (me + i) % n},
                            device_id_type=pl.DeviceIdType.MESH)
        return carry

    lax.fori_loop(1, n, tell, 0)
    pl.semaphore_wait(barrier, n - 1)

    col_tiles = acc.shape[0]
    tail = [min(LANES, cols - t * LANES) for t in range(col_tiles)]
    acc[...] = jnp.zeros_like(acc)

    def one_pair(i, carry):
        digits = carry
        slot = i % 2
        chips = tuple(chip_at(digits[2 * a] % side, digits[2 * a + 1] % side) for a in range(2))
        digits = tuple(d // side for d in digits)

        @pl.when(i + 1 < n_steps)
        def _():
            coming = tuple(chip_at(digits[2 * a] % side, digits[2 * a + 1] % side) for a in range(2))
            for k in range(slices):
                fetch(1 - slot, k, coming)

        def one_slice(k, c):
            pltpu.make_async_copy(hbuf.at[slot, :, pl.ds(0, span)], hbuf.at[slot, :, pl.ds(0, span)],
                                  hsem.at[slot, k]).wait()

            @pl.when(i == 0)
            def _():
                cut = pl.ds(0, span * LANES)
                pltpu.make_async_copy(wbuf.at[:, cut], wbuf.at[:, cut], wsem.at[k]).wait()

            x = jnp.concatenate([hbuf[slot, :, k * span + u].reshape(rows, LANES) for u in range(span)], axis=1)
            w = wbuf[:, pl.ds(pl.multiple_of(k * span * LANES, span * LANES), span * LANES)]
            z = lax.dot_general(x, w, (((1,), (1,)), ((), ())), preferred_element_type=jnp.float32)
            for t in range(col_tiles):
                acc[t, :, :tail[t]] += z[:, t * LANES:t * LANES + tail[t]]
            return c

        lax.fori_loop(0, slices, one_slice, 0)

        def code_rows(d, c):
            for j in range(pos):
                z = jnp.concatenate([acc[t, pl.ds(d * dev_rows + j, blk_seqs, stride=pos), :]
                                     for t in range(col_tiles)], axis=1) * INV_TEMP
                live = z[:, :cols]
                peak = jnp.max(live, axis=1, keepdims=True)
                low = jnp.min(live, axis=1, keepdims=True)
                width = jnp.clip(peak - low, 1e-30, MAX_SPAN)
                mass = jnp.sum(jnp.exp(live - peak), axis=1, keepdims=True)
                code = jnp.clip((peak - z) * (TOP_CODE / width), 0.0, TOP_CODE) + 0.5
                code = code.astype(jnp.int32)
                sbuf[i * 2 * cores + d, j * blk_seqs:(j + 1) * blk_seqs, :] = (
                    code[:, :half] | (code[:, half:] << 16))
                lane = lax.broadcasted_iota(jnp.int32, (blk_seqs, LANES), 1)
                stat = jnp.where(lane == 0, peak, jnp.where(lane == 1, width * (1.0 / TOP_CODE), mass))
                stcol[pl.ds(pl.multiple_of(d * dev_rows + j * blk_seqs, blk_seqs), blk_seqs), :] = stat
            return c

        lax.fori_loop(0, 2 * cores, code_rows, 0)
        acc[...] = jnp.zeros_like(acc)
        for a in range(2):
            flat = stcol[a * LANES:(a + 1) * LANES, :].T
            stbuf[2 * i + a] = flat[:8]

        for d in range(2 * cores):
            dest = chips[d // cores] * cores + d % cores
            src = sbuf.at[i * 2 * cores + d]
            stat_src = stbuf.at[2 * i + d // cores]

            @pl.when(dest == me)
            def _():
                pltpu.make_async_copy(src, code_ref.at[me], self_sem.at[0]).start()
                pltpu.make_async_copy(stat_src, stat_ref.at[me], self_sem.at[1]).start()

            @pl.when(dest != me)
            def _():
                pltpu.make_async_remote_copy(src, code_ref.at[me], code_send, code_recv, device_id={tp: dest},
                                             device_id_type=pl.DeviceIdType.MESH).start()
                pltpu.make_async_remote_copy(stat_src, stat_ref.at[me], stat_send, stat_recv, device_id={tp: dest},
                                             device_id_type=pl.DeviceIdType.MESH).start()

        return digits

    lax.fori_loop(0, n_steps, one_pair, tuple(jnp.int32(t) for t in tables))

    others = pl.ds(0, n - 1)
    pltpu.make_async_copy(code_ref.at[0], code_ref.at[0], self_sem.at[0]).wait()
    pltpu.make_async_copy(stat_ref.at[0], stat_ref.at[0], self_sem.at[1]).wait()
    for sem in (code_send, code_recv):
        pltpu.make_async_copy(code_ref.at[others], code_ref.at[others], sem).wait()
    for sem in (stat_send, stat_recv):
        pltpu.make_async_copy(stat_ref.at[others], stat_ref.at[others], sem).wait()


def exchange_logits(n, tp, hidden, w_shard):
    seqs, pos, depth = hidden.shape
    cols = w_shard.shape[1]
    tiles = depth // LANES
    half = pl.cdiv(cols, 2 * LANES) * LANES
    dev_rows = seqs // n * pos
    slices = 4
    h_tiles = hidden.reshape(seqs, pos, tiles, LANES).transpose(0, 2, 1, 3)
    blk = 4 * dev_rows
    return pl.pallas_call(
        functools.partial(logits_kernel, n, tp),
        out_shape=(jax.ShapeDtypeStruct((n, dev_rows, half), jnp.int32),
                   jax.ShapeDtypeStruct((n, 8, LANES), jnp.float32)),
        in_specs=[pl.BlockSpec(memory_space=pl.ANY)] * 2,
        out_specs=(pl.BlockSpec(memory_space=pl.ANY),) * 2,
        scratch_shapes=[
            pltpu.VMEM((cols, depth), jnp.bfloat16),
            pltpu.VMEM((2, blk // pos, tiles, pos, LANES), jnp.bfloat16),
            pltpu.VMEM((2 * half // LANES, blk, LANES), jnp.float32),
            pltpu.VMEM((n, dev_rows, half), jnp.int32),
            pltpu.VMEM((blk, LANES), jnp.float32),
            pltpu.VMEM((n // 2, 8, LANES), jnp.float32),
            pltpu.SemaphoreType.DMA((slices,)),
            pltpu.SemaphoreType.DMA((2, slices)),
            pltpu.SemaphoreType.DMA,
            pltpu.SemaphoreType.DMA,
            pltpu.SemaphoreType.DMA,
            pltpu.SemaphoreType.DMA,
            pltpu.SemaphoreType.DMA((2,)),
        ],
        compiler_params=pltpu.CompilerParams(collective_id=0, has_side_effects=True,
                                             vmem_limit_bytes=40 * 1024 * 1024),
        cost_estimate=pl.CostEstimate(flops=2 * seqs * pos * depth * cols,
                                      bytes_accessed=2 * (seqs * pos * depth + depth * cols), transcendentals=0),
        name="logits_exchange",
    )(h_tiles, w_shard.T)


def verify_kernel(n, tp, draft, code_ref, stat_ref, q_ref, x_ref, resid_ref, bonus_ref, accept_ref, expect_ref,
                  scale, prob, picks):
    g = pl.program_id(0)
    halves = prob_rows = 2
    me = lax.axis_index(tp)
    cols = prob.shape[1] // n
    half = code_ref.shape[2]
    own = code_ref.shape[1]
    width = prob.shape[1]
    lane = lax.broadcasted_iota(jnp.int32, (own, LANES), 1)
    sub = lax.broadcasted_iota(jnp.int32, (own, LANES), 0)

    @pl.when(g == 0)
    def _():
        mine = (me % 2) * (LANES // 2)
        turn = (LANES - mine) % LANES
        peak = pltpu.roll(stat_ref[:, 0, :], turn, 1)
        step = pltpu.roll(stat_ref[:, 1, :], turn, 1)
        mass = pltpu.roll(stat_ref[:, 2, :], turn, 1)
        top = jnp.max(peak, axis=0, keepdims=True)
        total = jnp.sum(mass * jnp.exp(peak - top), axis=0, keepdims=True)
        slope = step * (-LOG2E)
        base = (peak - top) * LOG2E - jnp.log(total) * LOG2E
        pad = jnp.zeros((LANES - 2 * n, LANES), jnp.float32)
        scale[...] = jnp.concatenate([slope, base, pad], axis=0).T
        picks[...] = jnp.zeros_like(picks)

    order = (g + (draft * halves)) % ((draft + 1) * halves)
    j = order // halves
    hb = order % halves
    row = scale[pl.ds(pl.multiple_of(order * own, own), own), :]
    for s in range(n):
        word = code_ref[s]
        low = (word & 0xFFFF).astype(jnp.float32)
        high = lax.shift_right_logical(word, 16).astype(jnp.float32)
        slope = row[:, s:s + 1]
        base = row[:, n + s:n + s + 1]
        both = jnp.concatenate([low, high], axis=1)
        prob[:, s * cols:(s + 1) * cols] = jnp.exp2(both * slope + base)[:, :cols]

    parts = 25
    part = width // parts

    @pl.when(j == draft)
    def _():
        def move(t, c):
            at = pl.ds(pl.multiple_of(t * part, LANES), part)
            bonus_ref[:, at] = prob[:, at]
            return c
        lax.fori_loop(0, parts, move, 0)

    @pl.when(j != draft)
    def _():
        names = jnp.broadcast_to(x_ref[pl.ds(j, 1), :], (own, x_ref.shape[1]))
        at_row = lax.broadcasted_iota(jnp.int32, names.shape, 1) == (
            lax.broadcasted_iota(jnp.int32, names.shape, 0) + me * (halves * own) + hb * own)
        name = jnp.sum(jnp.where(at_row, names, 0), axis=1, keepdims=True)
        wanted = name - lane

        def weigh(t, c):
            total, p_pick, q_pick = c
            for u in range(part // LANES):
                start = pl.multiple_of(t * part + u * LANES, LANES)
                p = prob[:, pl.ds(start, LANES)]
                q = q_ref[0, :, pl.ds(start, LANES)]
                over = jnp.maximum(p - q, 0.0)
                resid_ref[0, :, pl.ds(start, LANES)] = over
                total = total + over
                hit = wanted == start
                p_pick = jnp.where(hit, p, p_pick)
                q_pick = jnp.where(hit, q, q_pick)
            return total, p_pick, q_pick

        zero = jnp.zeros((own, LANES), jnp.float32)
        total, p_pick, q_pick = lax.fori_loop(0, parts, weigh, (zero, zero, zero))
        share = 1.0 / jnp.sum(total, axis=1, keepdims=True)

        def rescale(t, c):
            at = pl.ds(pl.multiple_of(t * part, LANES), part)
            resid_ref[0, :, at] = resid_ref[0, :, at] * share
            return c
        lax.fori_loop(0, parts, rescale, 0)

        ratio = jnp.sum(p_pick, axis=1, keepdims=True) / jnp.sum(q_pick, axis=1, keepdims=True)
        taken = jnp.minimum(1.0, ratio)
        spread = jnp.sum(jnp.where(lane == sub + hb * own, taken, 0.0), axis=0, keepdims=True)
        picks[pl.ds(j, 1), :] = picks[pl.ds(j, 1), :] + spread

    @pl.when(g == pl.num_programs(0) - 1)
    def _():
        run = jnp.ones((1, LANES), jnp.float32)
        tally = jnp.zeros((1, LANES), jnp.float32)
        for d in range(draft):
            run = run * picks[d:d + 1, :]
            tally = tally + run
        accept_ref[...] = picks[:draft, :halves * own]
        expect_ref[...] = tally[:, :halves * own]


def verify(n, tp, codes, stats, q_rows, x_group):
    seq_dev, draft, vocab = q_rows.shape
    half = codes.shape[2]
    own = 8
    halves = seq_dev // own
    q_by_pos = q_rows.transpose(1, 0, 2)
    x_by_pos = x_group.T
    last = (draft + 1) * halves
    spot = lambda g: (g + draft * halves) % last
    at_draft = lambda g: jnp.maximum(g - halves, 0)
    resid, bonus, accept, expect = pl.pallas_call(
        functools.partial(verify_kernel, n, tp, draft),
        grid=(last,),
        out_shape=(jax.ShapeDtypeStruct((draft, seq_dev, vocab), jnp.float32),
                   jax.ShapeDtypeStruct((seq_dev, vocab), jnp.float32),
                   jax.ShapeDtypeStruct((draft, seq_dev), jnp.float32),
                   jax.ShapeDtypeStruct((1, seq_dev), jnp.float32)),
        in_specs=[pl.BlockSpec((n, own, half), lambda g: (0, spot(g), 0)),
                  pl.BlockSpec(stats.shape, lambda g: (0, 0, 0)),
                  pl.BlockSpec((1, own, vocab), lambda g: (at_draft(g) // halves, at_draft(g) % halves, 0)),
                  pl.BlockSpec(x_by_pos.shape, lambda g: (0, 0))],
        out_specs=(pl.BlockSpec((1, own, vocab), lambda g: (at_draft(g) // halves, at_draft(g) % halves, 0)),
                   pl.BlockSpec((own, vocab), lambda g: (jnp.minimum(g, halves - 1), 0)),
                   pl.BlockSpec((draft, seq_dev), lambda g: (0, 0)),
                   pl.BlockSpec((1, seq_dev), lambda g: (0, 0))),
        scratch_shapes=[pltpu.VMEM((LANES, LANES), jnp.float32),
                        pltpu.VMEM((own, vocab), jnp.float32),
                        pltpu.VMEM((8, LANES), jnp.float32)],
        compiler_params=pltpu.CompilerParams(dimension_semantics=("arbitrary",),
                                             vmem_limit_bytes=32 * 1024 * 1024),
        name="verify_rows",
    )(codes, stats, q_by_pos, x_by_pos)
    return accept.T, expect[0], resid.transpose(1, 0, 2), bonus


def solution(mesh):
    n = mesh.shape["tp"]

    def local_step(hidden, w_shard, q_rows, x_group):
        codes, stats = exchange_logits(n, "tp", hidden, w_shard)
        return verify(n, "tp", codes, stats, q_rows, x_group)

    return jax.shard_map(local_step, mesh=mesh,
                         in_specs=(P("dp", None, None), P(None, "tp"), P(("dp", "tp"), None, None), P("dp", None)),
                         out_specs=(P(("dp", "tp"), None), P(("dp", "tp")), P(("dp", "tp"), None, None), P(("dp", "tp"), None)),
                         check_vma=False)
```

time: 269 us -> 94.3 us (0.35)
  the two profiles are of different devices: /device:TPU:103 before, /device:TPU:97 now
where the time goes in v1:
time: 94.3 us; the launch traced here: 94.2 us
  Pallas kernels  93.5 us (99%)
    pallas_call x1, Pallas kernels, exchange_logits(): pl.pallas_call(functools.partial(logits_kernel, n, tp), out_shape=(jax.Sh...  71.2 us
    pallas_call x1, Pallas kernels, verify(): pl.pallas_call(functools.partial(verify_kernel, n, tp, draft), grid=(last...  22.3 us

profile of v1, /device:TPU:97, one launch (start us, length us, event | category | flops | bytes accessed | tf_op | source)
XLA Modules:
  0.0 94.2 jit_solution(2201899204698132072)
XLA Ops:
  0.6 0.0 copy-start
  0.6 0.0 copy-start.1
  0.7 71.2 %logits_exchange.1 = (s32[32,64,512]{2,1,0:T(8,128)S(1)}, f32[32,8,128]{2,1,0:T(8,128)S(1)}) custom-call(bf16[512,64,4,128]{3,2,1,0:T(4,128)(2,1)} %bitcast.11, bf16[1000,8192]{1,0:T(8,128)(2,1)} %bitcast.12), custom_call_target="tpu_custom_call" | custom-call | flops 33554432000 | bytes 49938432 | tf_op jit(solution)/shard_map/logits_exchange/pallas_call | solution.py:179
  71.9 0.0 copy-done
  71.9 0.0 copy-done.1
  71.9 22.3 %verify_rows.1 = (f32[3,16,32000]{2,1,0:T(8,128)}, f32[16,32000]{1,0:T(8,128)}, f32[3,16]{1,0:T(4,128)}, f32[1,16]{1,0:T(1,128)}) custom-call(s32[32,64,512]{2,1,0:T(8,128)S(1)} %get-tuple-element.10.code_ref, f32[32,8,128]{2,1,0:T(8,128)S(1)} %get-tuple-element.11.stat_ref, f32[3,16,32000]{2,1,0:T(8,128)S(1)} %bitcast.9, s32[3,512]{1,0:T(4,128)S(1)} %bitcast.10), custom_call_target="tpu_custom_call" | custom-call | tf_op jit(solution)/shard_map/verify_rows/pallas_call | solution.py:317
Async XLA Ops:
  0.6 71.2 %copy-start = (f32[16,3,32000]{2,0,1:T(8,128)S(1)}, f32[16,3,32000]{2,0,1:T(8,128)}, u32[]{:S(2)}) copy-start(f32[16,3,32000]{2,0,1:T(8,128)} %param.6) | copy-start | bytes 18432004
  0.6 71.2 %copy-start.1 = (s32[512,3]{0,1:T(4,128)S(1)}, s32[512,3]{0,1:T(4,128)}, u32[]{:S(2)}) copy-start(s32[512,3]{0,1:T(4,128)} %param.7) | copy-start | bytes 18436
